TPU v7x, 512 devices: a whole 4x8x8 slice. The times are simulated.
512 devices in a mesh: tm: 8 (over x, core), src: 64 (over y, z).
Axes of the slice: x: 4, y: 8, z: 8, core: 2. Of those that a mesh axis runs over, the one named last changes fastest.
Arguments:
- design: float32 [16, 8388608], P(None, ('tm', 'src')), may hold values from -2 to 2
- unit_index: int32 [8388608], P(('tm', 'src')), may hold values from 0 to 4095, as said below
- residual: float32 [8388608], P(('tm', 'src')), may hold values from -6 to 6
- weight: float32 [8388608], P(('tm', 'src')), may hold values from 0.25 to 4
- obs_count: int32 [512], P(('tm', 'src')), may hold values from 1 to 16384, as said below
- damping: float32 [4096], P(('tm', 'src')), may hold values from 1 to 10
Outputs:
- solution: float32 [16, 4096], P(None, ('tm', 'src'))
- misfit: float32 [], replicated
Inputs may be any that keep to these rules, and one draw needn't show every extreme that they name: `unit_index`: an observation on a device of tm index g names a unit in [g * 512, (g + 1) * 512). `obs_count`: some device has all 16384 slots live.
All inputs are finite; a program needn't handle non-finite values.
Results may differ from a plain program's by a relative error of at most 0.0003.
Values sent between devices are 32-bit elements; how exact they have to be, the bound alone decides.
A program may use at most 64 MiB of HBM per device.

v0:
```python
import jax
import jax.numpy as jnp
from jax import lax
from jax.sharding import Mesh
from jax.sharding import PartitionSpec as P

SRC = ("src_0", "src_1")
TM = ("tm_0", "tm_1")
TM_SRC = ("tm_0", "tm_1", "src_0", "src_1")


def in_blocks(x, dim, devices):
    dims = x.shape
    pieces = x.reshape(*dims[:dim], devices, dims[dim] // devices, *dims[dim + 1 :])
    return jnp.moveaxis(pieces, dim, 0)


def summed_on_arrival(x, axis, dim):
    pieces = in_blocks(x, dim, lax.axis_size(axis))
    arrived = lax.all_to_all(pieces, axis, split_axis=0, concat_axis=0, tiled=True)
    return arrived.sum(axis=0)


def by_axis(x, axes):
    for axis in axes:
        x = lax.psum(x, axis)
    return x


def make_reader(stacked):

    def reader(row, column):
        return stacked[row * 16 + column]

    return reader


def block_solve(reader, rhs, damping):
    lower = {}
    for j in range(16):
        running = reader(j, j) + damping
        for k in range(j):
            running = running - lower[j, k] * lower[j, k]
        diag_term = jnp.sqrt(running)
        lower[j, j] = diag_term
        for i in range(j + 1, 16):
            running = reader(i, j)
            for k in range(j):
                running = running - lower[i, k] * lower[j, k]
            lower[i, j] = running / diag_term
    forward = []
    for i in range(16):
        running = rhs[i]
        for k in range(i):
            running = running - lower[i, k] * forward[k]
        forward.append(running / lower[i, i])
    backward = [None] * 16
    for i in range(15, -1, -1):
        running = forward[i]
        for k in range(i + 1, 16):
            running = running - lower[k, i] * backward[k]
        backward[i] = running / lower[i, i]
    return jnp.stack(backward)


def quadratic_terms(reader, rhs, solution_own):
    quadratic = jnp.zeros((), jnp.float32)
    for i in range(16):
        applied = jnp.zeros_like(solution_own[0])
        for j in range(16):
            applied = applied + reader(max(i, j), min(i, j)) * solution_own[j]
        quadratic = quadratic + jnp.sum(solution_own[i] * applied)
    return quadratic - 2.0 * jnp.sum(solution_own * rhs)


def on_device(design, unit_index, residual, weight, obs_count, damping):
    n_source = lax.axis_size(SRC)
    own_units = damping.shape[0]
    units_group = own_units * n_source
    slots = design.shape[1]
    local_unit = unit_index - lax.axis_index(TM) * units_group
    weights_on = jnp.where(
        jnp.arange(slots, dtype=jnp.int32) < obs_count[0], weight, jnp.zeros_like(weight)
    )
    block_rows = 1024
    turns = slots // block_rows
    pair_count = 256

    def pair_rows(rows):
        return (rows[:, None, :] * rows[None, :, :]).reshape(256, rows.shape[1])

    unit_range = jnp.arange(units_group, dtype=jnp.int32)

    def accumulate(step, partial_value):
        begin = step * block_rows
        rows = lax.dynamic_slice_in_dim(design, begin, block_rows, 1)
        units_of = lax.dynamic_slice_in_dim(local_unit, begin, block_rows, 0)
        resid = lax.dynamic_slice_in_dim(residual, begin, block_rows, 0)
        weights_blk = lax.dynamic_slice_in_dim(weights_on, begin, block_rows, 0)
        stacked = jnp.concatenate(
            [pair_rows(rows) * weights_blk, rows * (weights_blk * resid)], axis=0
        )
        one_hot = (units_of[:, None] == unit_range[None, :]).astype(jnp.float32)
        return partial_value + jnp.dot(
            stacked, one_hot, precision=lax.Precision.HIGHEST, preferred_element_type=jnp.float32
        )

    start = jnp.zeros((pair_count + 16, units_group), jnp.float32)
    partial_value = lax.fori_loop(0, turns, accumulate, start)
    own_part = summed_on_arrival(partial_value, SRC, 1)
    solution_own = block_solve(make_reader(own_part), own_part[pair_count:], damping)
    unit_terms = quadratic_terms(make_reader(own_part), own_part[pair_count:], solution_own)
    before = jnp.sum(weights_on * residual * residual)
    chi_total, weight_total = (
        by_axis(before + unit_terms, TM_SRC),
        by_axis(jnp.sum(weights_on), TM_SRC),
    )
    return (solution_own, chi_total / weight_total)


def solution(mesh):
    torus = Mesh(mesh.devices.reshape(4, 2, 8, 8), ("tm_0", "tm_1", "src_0", "src_1"))
    return jax.shard_map(
        on_device,
        mesh=torus,
        in_specs=(P(None, TM_SRC), P(TM_SRC), P(TM_SRC), P(TM_SRC), P(TM_SRC), P(TM_SRC)),
        out_specs=(P(None, TM_SRC), P()),
        check_vma=False,
    )
```

profile of v0, /device:TPU:8, one launch (start us, length us, event | category | flops | bytes accessed | tf_op | source)
XLA Modules:
  0.0 174.0 jit_solution(1141471634184720458)
XLA Ops:
  2.1 1.6 fusion.12
  3.7 52.6 %while.14 = (s32[]{:T(128)}, f32[272,512]{1,0:T(8,128)S(1)}, f32[16,16384]{1,0:T(8,128)}, f32[16384]{0:T(1024)S(1)}, f32[16384]{0:T(1024)}, /*index=5*/s32[16384...) while((s32[]{:T(128)}, f32[272,512]{1,0:T(8,128)S(1)}, f32[16,16384]{1,0:T(8,128)}, ...), condition=%wide.region_1.2_spmd.clone, body=%wide.region_0.1_spmd.clone.sunk | while | flops 1712899072 | bytes 5673129 | solution.py:109
  4.4 0.8 broadcast_multiply_fusion.4
  5.5 1.4 fusion.17
  7.7 0.8 broadcast_multiply_fusion.4
  8.8 1.4 fusion.17
  11.0 0.8 broadcast_multiply_fusion.4
  12.1 1.4 fusion.17
  15.4 1.4 fusion.17
  17.6 0.8 broadcast_multiply_fusion.4
  18.7 1.4 fusion.17
  20.8 0.8 broadcast_multiply_fusion.4
  22.0 1.4 fusion.17
  24.1 0.8 broadcast_multiply_fusion.4
  25.3 1.4 fusion.17
  27.4 0.8 broadcast_multiply_fusion.4
  28.6 1.4 fusion.17
  30.7 0.8 broadcast_multiply_fusion.4
  31.8 1.4 fusion.17
  35.1 1.4 fusion.17
  38.4 1.4 fusion.17
  41.7 1.4 fusion.17
  45.0 1.4 fusion.17
  48.3 1.4 fusion.17
  51.6 1.4 fusion.17
  54.9 1.4 fusion.17
  56.6 40.2 %all_to_all.5 = f32[64,272,8]{1,2,0:T(8,128)S(1)} all-to-all(f32[64,272,8]{1,2,0:T(8,128)S(1)} %bitcast.25), channel_id=1, replica_groups=mesh['tm_0'=4,'tm_1'=2,'src_0'=8,'src_1'=8] {'src_0','src_1'}, dimensions={0} | all-to-all | bytes 1114112 | tf_op jit(solution)/shard_map/all_to_all | solution.py:20
  101.6 0.9 multiply_reduce_fusion
  125.5 11.0 %all-reduce.2 = (f32[]{:T(128)}, f32[]{:T(128)}) all-reduce(f32[]{:T(128)S(6)} %add.1140, f32[]{:T(128)} %get-tuple-element.154), channel_id=1, replica_groups=mesh['tm_0'=4,'tm_1'=2,'src_0'=8,'src_1'=8] {'tm_0'}, use_global_device_ids=true, to_apply=%region_21.22 | all-reduce | flops 2 | bytes 16 | tf_op jit(solution)/shard_map/psum | solution.py:26
  136.5 3.2 %all-reduce.3 = (f32[]{:T(128)}, f32[]{:T(128)}) all-reduce(f32[]{:T(128)} %get-tuple-element.324, f32[]{:T(128)} %get-tuple-element.325), channel_id=1, replica_groups=mesh['tm_0'=4,'tm_1'=2,'src_0'=8,'src_1'=8] {'tm_1'}, use_global_device_ids=true, to_apply=%region_22.23 | all-reduce | flops 2 | bytes 16 | tf_op jit(solution)/shard_map/psum | solution.py:26
  139.7 16.0 %all-reduce.1 = (f32[]{:T(128)}, f32[]{:T(128)}) all-reduce(f32[]{:T(128)} %get-tuple-element.326, f32[]{:T(128)} %get-tuple-element.327), channel_id=1, replica_groups=mesh['tm_0'=4,'tm_1'=2,'src_0'=8,'src_1'=8] {'src_0'}, use_global_device_ids=true, to_apply=%region_23.24 | all-reduce | flops 2 | bytes 16 | tf_op jit(solution)/shard_map/psum | solution.py:26
  155.7 15.8 %all-reduce = (f32[]{:T(128)}, f32[]{:T(128)}) all-reduce(f32[]{:T(128)} %get-tuple-element.322, f32[]{:T(128)} %get-tuple-element.323), channel_id=1, replica_groups=mesh['tm_0'=4,'tm_1'=2,'src_0'=8,'src_1'=8] {'src_1'}, use_global_device_ids=true, to_apply=%region_24.25 | all-reduce | flops 2 | bytes 16 | tf_op jit(solution)/shard_map/psum | solution.py:26
  (123 shorter events, 39.7 us)
Async XLA Ops:
  96.8 4.2 %copy-start.1 = (f32[8]{0:T(128)S(1)}, f32[8]{0:T(128)}, u32[]{:S(2)}) copy-start(f32[8]{0:T(128)} %param.13) | copy-start | bytes 100
  113.8 59.1 %copy-start = (f32[16,8]{0,1:T(8,128)}, f32[16,8]{0,1:T(8,128)S(1)}, u32[]{:S(2)}) copy-start(f32[16,8]{0,1:T(8,128)S(1)} %stack.67) | copy-start | bytes 1540
where the time goes:
time: 176 us; the launch traced here: 174 us
  blocking collectives  86.2 us (49%)
  other arithmetic  43.1 us (24%)
  matrix products  22.9 us (13%)
  between operations  15 us (9%)
  local copies, waits for them, and re-layouts  5.88 us (3%)
    psum x4, blocking collectives, by_axis(): x = lax.psum(x, axis)  46 us
    all_to_all x1, blocking collectives, summed_on_arrival(): lax.all_to_all(pieces, axis, split_axis=0, concat_axis=0, tiled=True)  40.2 us
    dot_general x16, matrix products, accumulate(): jnp.dot(stacked, one_hot, precision=lax.Precision.HIGHEST, preferred_elem...  22.9 us
    mul x16, other arithmetic, accumulate(): rows * (weights_blk * resid)  13.6 us
    mul x16, other arithmetic, accumulate(): weights_blk * resid  11.1 us
    reduce_sum x16, other arithmetic, quadratic_terms(): quadratic = quadratic + jnp.sum(solution_own[i] * applied)  10.8 us
    slice x7, local copies, waits for them, and re-layouts, block_solve(): running = rhs[i]  3.55 us

commit v1 on v0

v1 whole, which is shorter than its diff:
```python
import functools

import jax
import jax.numpy as jnp
from jax import lax
from jax.experimental import pallas as pl
from jax.experimental.pallas import tpu as pltpu
from jax.sharding import PartitionSpec as P

TM = "tm"
SRC = "src"
MESH = pl.DeviceIdType.MESH
W = 16
OWN = 8
BF = jnp.bfloat16
F32 = jnp.float32


def dest_of(m, me, ny, nz):
    own = (ny // 2) * nz + nz // 2
    n = ny * nz
    i = m + (m + (n - own)) // n
    dy = (i // nz + ny // 2) % ny
    dz = (i % nz + nz // 2) % nz
    y = (me // nz + dy) % ny
    z = (me % nz + dz) % nz
    return y * nz + z


def pair_row(i, j):
    s = j - i
    if s < 8:
        return False, s * W + i
    if s == 8:
        return True, i
    return False, (W - s) * W + j


def kernel(
    dims,
    design_ref, unit_ref, resid_ref, weight_ref, count_ref, damping_ref,
    sol_ref, misfit_ref,
    feat, main_acc, rest_acc, sums_acc, main_out, rest_out, main_in, rest_in,
    table, plane_msg, plane_in, tm_msg, tm_in,
    main_send, main_recv, rest_send, rest_recv, plane_send, plane_recv, tm_send, tm_recv,
):
    nt, ny, nz, units, slots, chunk = dims
    n = ny * nz
    me_t = lax.axis_index(TM)
    me_s = lax.axis_index(SRC)

    barrier = pltpu.get_barrier_semaphore()

    def greet(m, carry):
        pl.semaphore_signal(
            barrier, inc=1, device_id=(me_t, dest_of(m, me_s, ny, nz)), device_id_type=MESH
        )
        return carry

    lax.fori_loop(0, n - 1, greet, 0)
    for d in range(1, nt):
        pl.semaphore_signal(
            barrier, inc=1, device_id=((me_t + d) % nt, me_s), device_id_type=MESH
        )

    main_acc[...] = jnp.zeros_like(main_acc)
    rest_acc[...] = jnp.zeros_like(rest_acc)
    sums_acc[...] = jnp.zeros_like(sums_acc)
    feat[...] = jnp.zeros_like(feat)
    count = count_ref[...]
    base = me_t * units
    half = min(units, 256)

    def accumulate(c, carry):
        at = pl.ds(pl.multiple_of(c * chunk, chunk), chunk)
        d = design_ref[:, at]
        slot = lax.broadcasted_iota(jnp.int32, (1, chunk), 1) + c * chunk
        w = jnp.where(slot < count, weight_ref[:, at], 0.0)
        r = resid_ref[:, at]
        wr = w * r
        sums_acc[0:1, :] += wr * r
        sums_acc[1:2, :] += w
        u = unit_ref[:, at] - base
        wd = d * w

        def put(value, row):
            hi = value.astype(BF)
            lo = (value - hi.astype(F32)).astype(BF)
            k = value.shape[0]
            feat[row : row + k, :] = hi
            feat[128 + row : 128 + row + k, :] = lo

        for s in range(8):
            turned = d if s == 0 else pltpu.roll(d, W - s, 0)
            put(wd * turned, s * W)
        tail = jnp.concatenate([wd[:8] * d[8:], d * wr], axis=0)
        tail_hi = tail.astype(BF).astype(F32)
        tail_lo = tail - tail_hi
        quarter = (u // 2) % 4
        for q in range(4):
            on = quarter == q
            feat[256 + q * 32 : 256 + q * 32 + 32, :] = jnp.concatenate(
                [jnp.where(on, tail_hi, 0.0), jnp.zeros((8, chunk), F32)], axis=0
            ).astype(BF)
            feat[384 + q * 32 : 384 + q * 32 + 32, :] = jnp.concatenate(
                [jnp.where(on, tail_lo, 0.0), jnp.zeros((8, chunk), F32)], axis=0
            ).astype(BF)

        def one_hot(index, rows):
            lines = lax.broadcasted_iota(jnp.int32, (rows, chunk), 0).astype(F32).astype(BF)
            return jnp.where(lines == index.astype(F32).astype(BF), jnp.ones((), BF), jnp.zeros((), BF))

        dn = (((1,), (1,)), ((), ()))
        for h in range(units // half):
            main_acc[h * half : (h + 1) * half, :] += lax.dot_general(
                one_hot(u - h * half, half), feat[0:256, :], dn, preferred_element_type=F32
            )
        line = (u // 8) * 2 + u % 2
        rest_acc[...] += lax.dot_general(
            one_hot(line, units // 4), feat[256:512, :], dn, preferred_element_type=F32
        )
        return carry

    lax.fori_loop(0, slots // chunk, accumulate, 0)
    main_out[...] = (main_acc[:, 0:128] + main_acc[:, 128:256]).reshape(n, OWN, 128)
    rest_out[...] = (rest_acc[:, 0:128] + rest_acc[:, 128:256]).reshape(n, 2, 128)

    pl.semaphore_wait(barrier, n - 1 + nt - 1)

    def send(m, carry):
        dest = dest_of(m, me_s, ny, nz)
        pltpu.make_async_remote_copy(
            src_ref=main_out.at[dest], dst_ref=main_in.at[m],
            send_sem=main_send, recv_sem=main_recv,
            device_id=(me_t, dest), device_id_type=MESH,
        ).start()
        pltpu.make_async_remote_copy(
            src_ref=rest_out.at[dest], dst_ref=rest_in.at[m],
            send_sem=rest_send, recv_sem=rest_recv,
            device_id=(me_t, dest), device_id_type=MESH,
        ).start()
        return carry

    lax.fori_loop(0, n - 1, send, 0)
    before = jnp.sum(sums_acc[0:1, :], axis=1, keepdims=True)
    weight_sum = jnp.sum(sums_acc[1:2, :], axis=1, keepdims=True)

    pltpu.make_async_copy(rest_in, rest_in, rest_recv).wait()
    pltpu.make_async_copy(main_in, main_in, main_recv).wait()

    main = main_out[me_s] + jnp.sum(main_in[...], axis=0)
    rest = rest_out[me_s] + jnp.sum(rest_in[...], axis=0)
    table[0:128, :] = jnp.concatenate([main, jnp.zeros((120, 128), F32)], axis=0).T
    rest_t = jnp.concatenate([rest, jnp.zeros((126, 128), F32)], axis=0).T
    lane = lax.broadcasted_iota(jnp.int32, (24, 128), 1)
    rest_all = jnp.zeros((24, 128), F32)
    for q in range(4):
        piece = rest_t[q * 32 : q * 32 + 24, :]
        moved = piece if q == 0 else pltpu.roll(piece, 2 * q, 1)
        rest_all = jnp.where(lane // 2 == q, moved, rest_all)
    table[128:152, :] = rest_all

    def entry(i, j):
        is_rest, row = pair_row(i, j)
        row = row + 128 if is_rest else row
        return table[row : row + 1, 0:OWN]

    damping = damping_ref[...]
    a = {}
    for i in range(W):
        for j in range(i, W):
            a[i, j] = entry(i, j)
        a[i, i] = a[i, i] + damping
    b0 = [table[136 + i : 137 + i, 0:OWN] for i in range(W)]
    b = list(b0)
    inv = [None] * W
    for k in range(W):
        inv[k] = 1.0 / a[k, k]
        for j in range(k + 1, W):
            factor = a[k, j] * inv[k]
            for i in range(k + 1, j + 1):
                a[i, j] = a[i, j] - a[k, i] * factor
            b[j] = b[j] - factor * b[k]
    x = [None] * W
    for k in range(W - 1, -1, -1):
        x[k] = b[k] * inv[k]
        for i in range(k):
            b[i] = b[i] - a[i, k] * x[k]
    gain = jnp.zeros((1, OWN), F32)
    square = jnp.zeros((1, OWN), F32)
    for k in range(W):
        sol_ref[k : k + 1, :] = x[k]
        gain = gain + x[k] * b0[k]
        square = square + x[k] * x[k]
    chi = before - jnp.sum(gain + damping * square, axis=1, keepdims=True)

    lane_row = lax.broadcasted_iota(jnp.int32, (1, 128), 1)
    plane_msg[...] = jnp.where(lane_row == 0, chi, jnp.where(lane_row == 1, weight_sum, 0.0))

    def tell(m, carry):
        dest = dest_of(m, me_s, ny, nz)
        pltpu.make_async_remote_copy(
            src_ref=plane_msg, dst_ref=plane_in.at[m],
            send_sem=plane_send, recv_sem=plane_recv,
            device_id=(me_t, dest), device_id_type=MESH,
        ).start()
        return carry

    lax.fori_loop(0, n - 1, tell, 0)
    pltpu.make_async_copy(plane_in, plane_in, plane_recv).wait()
    tm_msg[...] = plane_msg[...] + jnp.sum(plane_in[...], axis=0)
    for d in range(1, nt):
        pltpu.make_async_remote_copy(
            src_ref=tm_msg, dst_ref=tm_in.at[d - 1],
            send_sem=tm_send, recv_sem=tm_recv,
            device_id=((me_t + d) % nt, me_s), device_id_type=MESH,
        ).start()
    pltpu.make_async_copy(tm_in, tm_in, tm_recv).wait()
    total = tm_msg[...] + jnp.sum(tm_in[...], axis=0)
    misfit_ref[...] = total[:, 0:1] / total[:, 1:2]

    pltpu.make_async_copy(main_in, main_in, main_send).wait()
    pltpu.make_async_copy(rest_in, rest_in, rest_send).wait()
    pltpu.make_async_copy(plane_in, plane_in, plane_send).wait()
    pltpu.make_async_copy(tm_in, tm_in, tm_send).wait()


def solution(mesh):
    nt = mesh.shape[TM]
    n = mesh.shape[SRC]
    nz = 8 if n == 64 else 2
    ny = n // nz
    units = n * OWN

    def on_device(design, unit_index, residual, weight, obs_count, damping):
        slots = design.shape[1]
        chunk = min(2048, slots // 2)
        dims = (nt, ny, nz, units, slots, chunk)
        vmem = pl.BlockSpec(memory_space=pltpu.VMEM)
        dma = pltpu.SemaphoreType.DMA
        sol, misfit = pl.pallas_call(
            functools.partial(kernel, dims),
            out_shape=(
                jax.ShapeDtypeStruct((W, OWN), F32),
                jax.ShapeDtypeStruct((1, 1), F32),
            ),
            in_specs=[vmem] * 6,
            out_specs=(vmem, vmem),
            scratch_shapes=[
                pltpu.VMEM((512, chunk), BF),
                pltpu.VMEM((units, 256), F32),
                pltpu.VMEM((units // 4, 256), F32),
                pltpu.VMEM((2, chunk), F32),
                pltpu.VMEM((n, OWN, 128), F32),
                pltpu.VMEM((n, 2, 128), F32),
                pltpu.VMEM((n - 1, OWN, 128), F32),
                pltpu.VMEM((n - 1, 2, 128), F32),
                pltpu.VMEM((152, 128), F32),
                pltpu.VMEM((1, 128), F32),
                pltpu.VMEM((n - 1, 1, 128), F32),
                pltpu.VMEM((1, 128), F32),
                pltpu.VMEM((nt - 1, 1, 128), F32),
            ] + [dma] * 8,
            compiler_params=pltpu.CompilerParams(collective_id=0, has_side_effects=True),
            name="calibrate",
        )(
            design,
            unit_index.reshape(1, slots),
            residual.reshape(1, slots),
            weight.reshape(1, slots),
            obs_count.reshape(1, 1),
            damping.reshape(1, OWN),
        )
        return sol, misfit.reshape(())

    both = P((TM, SRC))
    return jax.shard_map(
        on_device,
        mesh=mesh,
        in_specs=(P(None, (TM, SRC)), both, both, both, both, both),
        out_specs=(P(None, (TM, SRC)), P()),
        check_vma=False,
    )
```

time: 176 us -> 52.5 us (0.30)
  the two profiles are of different devices: /device:TPU:8 before, /device:TPU:1 now
where the time goes in v1:
time: 52.5 us; the launch traced here: 52.3 us
  Pallas kernels  47.9 us (91%)
  between operations  3.05 us (6%)
  local copies, waits for them, and re-layouts  1.36 us (3%)
    pallas_call x1, Pallas kernels, on_device(): pl.pallas_call(functools.partial(kernel, dims), out_shape=(jax.ShapeDtype...  47.9 us
    unnamed x1, local copies, waits for them, and re-layouts  1.36 us

profile of v1, /device:TPU:1, one launch (start us, length us, event | category | flops | bytes accessed | tf_op | source)
XLA Modules:
  0.0 52.3 jit_solution(6968406348673786918)
XLA Ops:
  1.3 47.9 %calibrate.1 = (f32[16,8]{1,0:T(8,128)}, f32[1,1]{1,0:T(1,128)}) custom-call(f32[16,16384]{1,0:T(8,128)} %design_ref.1, s32[1,16384]{1,0:T(1,128)} %bitcast.7, f32[1,16384]{1,0:T(1,128)} %bitcast.8, f32[1,16384]{1,0:T(1,128)} %bitcast.9, s32[1,1]{1,0:T(1,128)} %bitcast.6.count_ref, f32[1,8]{1,0:T(1,128)} %bitcast.10), custom_call_target="tpu_custom_call" | custom-call | tf_op jit(solution)/shard_map/calibrate/pallas_call | solution.py:241
  49.2 1.4 %copy.8 = f32[16,8]{0,1:T(8,128)} copy(f32[16,8]{1,0:T(8,128)} %get-tuple-element.6) | data formatting | bytes 1024

commit v2 on v1

v2 whole, which is shorter than its diff:
```python
import functools

import jax
import jax.numpy as jnp
from jax import lax
from jax.experimental import pallas as pl
from jax.experimental.pallas import tpu as pltpu
from jax.sharding import PartitionSpec as P

TM = "tm"
SRC = "src"
MESH = pl.DeviceIdType.MESH
W = 16
OWN = 8
BF = jnp.bfloat16
F32 = jnp.float32


def ring_hops(d, size):
    return min(d, size - d)


def far_first(ny, nz):
    every = [(dy, dz) for dy in range(ny) for dz in range(nz)]
    return sorted(every, key=lambda o: -(ring_hops(o[0], ny) + ring_hops(o[1], nz)))


def pair_row(i, j):
    s = j - i
    if s < 8:
        return False, s * W + i
    if s == 8:
        return True, W + i
    return False, (W - s) * W + j


def kernel(
    dims,
    design_hbm, unit_hbm, resid_hbm, weight_hbm, count_hbm, damping_hbm,
    sol_ref, misfit_ref,
    design_ref, unit_ref, resid_ref, weight_ref, count_ref, damping_ref,
    line_wide, lines, rest_lines,
    feat, rest_feat, main_acc, rest_acc, sums_acc, out_box, in_box,
    table, plane_msg, plane_in, tm_msg, tm_in,
    design_sem, row_sem, box_send, box_recv, plane_send, plane_recv, tm_send, tm_recv,
):
    nt, ny, nz, units, slots, chunk = dims
    n = ny * nz
    turns = slots // chunk
    half_units = units // 2
    half_boxes = n // 2
    me_t = lax.axis_index(TM)
    me_s = lax.axis_index(SRC)
    me_y = me_s // nz
    me_z = me_s % nz

    def piece(c):
        at = pl.ds(pl.multiple_of(c * chunk, chunk), chunk)
        return pltpu.make_async_copy(design_hbm.at[:, at], design_ref.at[:, at], design_sem.at[c])

    rows = [
        pltpu.make_async_copy(a, b, row_sem.at[i])
        for i, (a, b) in enumerate(
            [
                (count_hbm, count_ref), (weight_hbm, weight_ref), (resid_hbm, resid_ref),
                (unit_hbm, unit_ref), (damping_hbm, damping_ref),
            ]
        )
    ]
    for row in rows:
        row.start()
    for c in range(turns):
        piece(c).start()

    ys = [(me_y + d) % ny for d in range(ny)]
    zs = [(me_z + d) % nz for d in range(nz)]
    ts = [(me_t + d) % nt for d in range(nt)]
    order = far_first(ny, nz)

    def owner(o):
        return ys[o[0]] * nz + zs[o[1]]

    def peer(o):
        return (me_t, owner(o))

    barrier = pltpu.get_barrier_semaphore()
    for o in order[:-1]:
        pl.semaphore_signal(barrier, inc=1, device_id=peer(o), device_id_type=MESH)
    for d in range(1, nt):
        pl.semaphore_signal(barrier, inc=1, device_id=(ts[d], me_s), device_id_type=MESH)

    eight = lax.broadcasted_iota(jnp.int32, (OWN, 128), 0)
    for k, o in enumerate(order):
        line_wide[k * OWN : (k + 1) * OWN, :] = (eight + (owner(o) * OWN - 256)).astype(F32)
    lines[...] = line_wide[...].astype(BF)
    for k in range(0, n, 4):
        four = owner(order[k])
        for i in range(1, 4):
            four = jnp.where(eight // 2 == i, owner(order[k + i]), four)
        line_wide[2 * k : 2 * k + OWN, :] = (four * 2 + eight % 2).astype(F32)
    rest_lines[...] = line_wide[0 : 2 * n, :].astype(BF)

    main_acc[...] = jnp.zeros_like(main_acc)
    rest_acc[...] = jnp.zeros_like(rest_acc)
    sums_acc[...] = jnp.zeros_like(sums_acc)
    for row in rows:
        row.wait()
    count = count_ref[0]
    base = me_t * units

    dn = (((1,), (1,)), ((), ()))
    one, zero = jnp.ones((), BF), jnp.zeros((), BF)

    def hits(which, code):
        return jnp.where(
            jnp.concatenate([which] * (chunk // 128), axis=1) == code.astype(F32).astype(BF), one, zero
        )

    def split(value):
        hi = value.astype(BF)
        return hi, (value - hi.astype(F32)).astype(BF)

    def first_half(c, carry):
        at = pl.ds(pl.multiple_of(c * chunk, chunk), chunk)
        piece(c).wait()
        d = design_ref[:, at]
        slot = lax.broadcasted_iota(jnp.int32, (1, chunk), 1) + c * chunk
        w = jnp.where(slot < count, weight_ref[:, at], 0.0)
        r = resid_ref[:, at]
        wr = w * r
        sums_acc[0:1, :] += wr * r
        sums_acc[1:2, :] += w
        u = unit_ref[:, at] - base
        wd = d * w

        for s in range(8):
            turned = d if s == 0 else pltpu.roll(d, W - s, 0)
            hi, lo = split(wd * turned)
            feat[s * W : (s + 1) * W, at] = hi
            feat[128 + s * W : 128 + (s + 1) * W, at] = lo
        tail = jnp.concatenate([d * wr, wd[:8] * d[8:], jnp.zeros((8, chunk), F32)], axis=0)
        tail_hi, tail_lo = split(tail)
        quarter = (lax.shift_right_logical(u, 1) & 3).astype(F32).astype(BF)
        for q in range(4):
            on = quarter == jnp.asarray(q, BF)
            rest_feat[q * 32 : q * 32 + 32, :] = jnp.where(on, tail_hi, zero)
            rest_feat[128 + q * 32 : 160 + q * 32, :] = jnp.where(on, tail_lo, zero)

        code = u - 256
        unit_ref[:, at] = code
        main_acc[0:half_units, :] += lax.dot_general(
            hits(lines[0:half_units, :], code), feat[:, at], dn, preferred_element_type=F32
        )
        rest_code = (lax.shift_right_logical(u, 3) * 2) | (u & 1)
        rest_acc[...] += lax.dot_general(
            hits(rest_lines[...], rest_code), rest_feat[...], dn, preferred_element_type=F32
        )
        return carry

    def second_half(c, carry):
        at = pl.ds(pl.multiple_of(c * chunk, chunk), chunk)
        main_acc[half_units:units, :] += lax.dot_general(
            hits(lines[half_units:units, :], unit_ref[:, at]), feat[:, at], dn, preferred_element_type=F32
        )
        return carry

    def fill(h):
        got = main_acc[h * half_units : (h + 1) * half_units, :]
        out_box[h * half_boxes : (h + 1) * half_boxes, 0:4] = (
            got[:, 0:128] + got[:, 128:256]
        ).reshape(half_boxes, 4, 2, 128)

    def send(h):
        for k in range(h * half_boxes, min((h + 1) * half_boxes, n - 1)):
            pltpu.make_async_remote_copy(
                src_ref=out_box.at[k], dst_ref=in_box.at[k],
                send_sem=box_send.at[h], recv_sem=box_recv.at[h],
                device_id=peer(order[k]), device_id_type=MESH,
            ).start()

    halves = (in_box.at[0:half_boxes], in_box.at[half_boxes : n - 1])

    lax.fori_loop(0, turns, first_half, 0)
    out_box[:, 4:5] = (rest_acc[:, 0:128] + rest_acc[:, 128:256]).reshape(n, 1, 2, 128)
    fill(0)
    pl.semaphore_wait(barrier, n - 1 + nt - 1)
    send(0)
    lax.fori_loop(0, turns, second_half, 0)
    fill(1)
    send(1)

    before = jnp.sum(sums_acc[0:1, :], axis=1, keepdims=True)
    weight_sum = jnp.sum(sums_acc[1:2, :], axis=1, keepdims=True)
    damping = damping_ref[...]
    own = out_box[n - 1]
    pltpu.make_async_copy(halves[0], halves[0], box_recv.at[0]).wait()
    own = own + jnp.sum(in_box[0:half_boxes], axis=0)
    pltpu.make_async_copy(halves[1], halves[1], box_recv.at[1]).wait()
    own = own + jnp.sum(in_box[half_boxes : n - 1], axis=0)
    main = own[0:4].reshape(OWN, 128)
    rest = own[4]
    table[0:128, :] = jnp.concatenate([main, jnp.zeros((120, 128), F32)], axis=0).T
    rest_t = jnp.concatenate([rest, jnp.zeros((126, 128), F32)], axis=0).T
    lane = lax.broadcasted_iota(jnp.int32, (24, 128), 1)
    rest_all = jnp.zeros((24, 128), F32)
    for q in range(4):
        part = rest_t[q * 32 : q * 32 + 24, :]
        moved = part if q == 0 else pltpu.roll(part, 2 * q, 1)
        rest_all = jnp.where(lane // 2 == q, moved, rest_all)
    table[128:152, :] = rest_all

    def entry(i, j):
        is_rest, row = pair_row(i, j)
        row = row + 128 if is_rest else row
        return table[row : row + 1, 0:OWN]

    a = {}
    for i in range(W):
        for j in range(i, W):
            a[i, j] = entry(i, j)
        a[i, i] = a[i, i] + damping
    b0 = [table[128 + i : 129 + i, 0:OWN] for i in range(W)]
    b = list(b0)
    inv = [None] * W
    for k in range(W):
        inv[k] = 1.0 / a[k, k]
        for j in range(k + 1, W):
            factor = a[k, j] * inv[k]
            for i in range(k + 1, j + 1):
                a[i, j] = a[i, j] - a[k, i] * factor
            b[j] = b[j] - factor * b[k]
    x = [None] * W
    for k in range(W - 1, -1, -1):
        x[k] = b[k] * inv[k]
        for i in range(k):
            b[i] = b[i] - a[i, k] * x[k]
    gain = jnp.zeros((1, OWN), F32)
    square = jnp.zeros((1, OWN), F32)
    for k in range(W):
        gain = gain + x[k] * b0[k]
        square = square + x[k] * x[k]
    chi = before - jnp.sum(gain + damping * square, axis=1, keepdims=True)

    lane_row = lax.broadcasted_iota(jnp.int32, (1, 128), 1)
    plane_msg[...] = jnp.where(lane_row == 0, chi, jnp.where(lane_row == 1, weight_sum, 0.0))

    for m, o in enumerate(order[:-1]):
        pltpu.make_async_remote_copy(
            src_ref=plane_msg, dst_ref=plane_in.at[m],
            send_sem=plane_send, recv_sem=plane_recv,
            device_id=peer(o), device_id_type=MESH,
        ).start()
    for k in range(W):
        table[k : k + 1, 0:OWN] = x[k]
    sol_ref[...] = table[...].T[0:OWN, 0:W]
    pltpu.make_async_copy(plane_in, plane_in, plane_recv).wait()
    tm_msg[...] = plane_msg[...] + jnp.sum(plane_in[...], axis=0)
    for d in range(1, nt):
        pltpu.make_async_remote_copy(
            src_ref=tm_msg, dst_ref=tm_in.at[d - 1],
            send_sem=tm_send, recv_sem=tm_recv,
            device_id=(ts[d], me_s), device_id_type=MESH,
        ).start()
    for h in range(2):
        pltpu.make_async_copy(halves[h], halves[h], box_send.at[h]).wait()
    pltpu.make_async_copy(plane_in, plane_in, plane_send).wait()
    pltpu.make_async_copy(tm_in, tm_in, tm_recv).wait()
    total = tm_msg[...] + jnp.sum(tm_in[...], axis=0)
    misfit_ref[...] = total[:, 0:1] / total[:, 1:2]
    pltpu.make_async_copy(tm_in, tm_in, tm_send).wait()


def solution(mesh):
    nt = mesh.shape[TM]
    n = mesh.shape[SRC]
    nz = 8 if n == 64 else 2
    ny = n // nz
    units = n * OWN

    def on_device(design, unit_index, residual, weight, obs_count, damping):
        slots = design.shape[1]
        chunk = min(2048, slots // 2)
        dims = (nt, ny, nz, units, slots, chunk)
        vmem = pl.BlockSpec(memory_space=pltpu.VMEM)
        hbm = pl.BlockSpec(memory_space=pl.ANY)
        dma = pltpu.SemaphoreType.DMA
        sol, misfit = pl.pallas_call(
            functools.partial(kernel, dims),
            out_shape=(
                pltpu.VMEM((OWN, W), F32),
                pltpu.VMEM((1, 1), F32),
            ),
            in_specs=[hbm] * 6,
            out_specs=(vmem, vmem),
            scratch_shapes=[
                pltpu.VMEM((W, slots), F32),
                pltpu.VMEM((1, slots), jnp.int32),
                pltpu.VMEM((1, slots), F32),
                pltpu.VMEM((1, slots), F32),
                pltpu.SMEM((1,), jnp.int32),
                pltpu.VMEM((1, OWN), F32),
                pltpu.VMEM((units, 128), F32),
                pltpu.VMEM((units, 128), BF),
                pltpu.VMEM((units // 4, 128), BF),
                pltpu.VMEM((256, slots), BF),
                pltpu.VMEM((256, chunk), BF),
                pltpu.VMEM((units, 256), F32),
                pltpu.VMEM((units // 4, 256), F32),
                pltpu.VMEM((2, chunk), F32),
                pltpu.VMEM((n, 5, 2, 128), F32),
                pltpu.VMEM((n, 5, 2, 128), F32),
                pltpu.VMEM((152, 128), F32),
                pltpu.VMEM((1, 128), F32),
                pltpu.VMEM((n - 1, 1, 128), F32),
                pltpu.VMEM((1, 128), F32),
                pltpu.VMEM((nt - 1, 1, 128), F32),
                dma((slots // chunk,)),
                dma((5,)),
                dma((2,)),
                dma((2,)),
                dma, dma, dma, dma,
            ],
            compiler_params=pltpu.CompilerParams(collective_id=0, has_side_effects=True),
            name="calibrate",
        )(
            design,
            unit_index.reshape(1, slots),
            residual.reshape(1, slots),
            weight.reshape(1, slots),
            obs_count,
            damping.reshape(1, OWN),
        )
        return sol.T, misfit.reshape(())

    both = P((TM, SRC))
    return jax.shard_map(
        on_device,
        mesh=mesh,
        in_specs=(P(None, (TM, SRC)), both, both, both, both, both),
        out_specs=(P(None, (TM, SRC)), P()),
        check_vma=False,
    )
```

time: 52.5 us -> 43.8 us (0.83)
  Pallas kernels: 47.9 us -> 40.6 us
  local copies, waits for them, and re-layouts: 1.36 us -> 0.6 us
  between operations: 3.05 us -> 2.45 us
    pallas_call x1, Pallas kernels: 47.9 us -> 40.6 us  [on_device(): pl.pallas_call(functools.partial(kernel, dims), out_shape=(pltpu.VMEM((OW...]
    unnamed x1, local copies, waits for them, and re-layouts: 1.36 us -> 0.6 us
where the time goes in v2:
time: 43.8 us; the launch traced here: 43.6 us
  Pallas kernels  40.6 us (93%)
  between operations  2.45 us (6%)
  local copies, waits for them, and re-layouts  0.6 us (1%)
    pallas_call x1, Pallas kernels, on_device(): pl.pallas_call(functools.partial(kernel, dims), out_shape=(pltpu.VMEM((OW...  40.6 us

profile of v2, /device:TPU:1, one launch (start us, length us, event | category | flops | bytes accessed | tf_op | source)
XLA Modules:
  0.0 43.6 jit_solution(12090564517943085234)
XLA Ops:
  1.3 40.6 %calibrate.1 = (f32[8,16]{1,0:T(8,128)S(1)}, f32[1,1]{1,0:T(1,128)S(1)}) custom-call(f32[16,16384]{1,0:T(8,128)} %design_hbm.1, s32[1,16384]{1,0:T(1,128)} %bitcast.7, f32[1,16384]{1,0:T(1,128)} %bitcast.8, f32[1,16384]{1,0:T(1,128)} %bitcast.9, s32[1]{0:T(128)S(6)} %copy.12.count_hbm, f32[1,8]{1,0:T(1,128)} %bitcast.10), custom_call_target="tpu_custom_call" | custom-call | tf_op jit(solution)/shard_map/calibrate/pallas_call | solution.py:287
  41.9 0.6 %copy.10 = f32[16,8]{0,1:T(8,128)} copy(f32[16,8]{0,1:T(8,128)S(1)} %bitcast.6) | data formatting | bytes 1024

commit v3 on v2

--- a/solution.py
+++ b/solution.py
@@ -86,8 +86,18 @@
     barrier = pltpu.get_barrier_semaphore()
     for o in order[:-1]:
         pl.semaphore_signal(barrier, inc=1, device_id=peer(o), device_id_type=MESH)
-    for d in range(1, nt):
-        pl.semaphore_signal(barrier, inc=1, device_id=(ts[d], me_s), device_id_type=MESH)
+    root_z = 1
+    served = nz // root_z - 1
+    is_root = me_z < root_z
+
+    @pl.when(is_root)
+    def _():
+        def greet(place, carry):
+            for d in range(1, nt):
+                pl.semaphore_signal(barrier, inc=1, device_id=(ts[d], place), device_id_type=MESH)
+            return carry
+
+        lax.fori_loop(0, n, greet, 0)
 
     eight = lax.broadcasted_iota(jnp.int32, (OWN, 128), 0)
     for k, o in enumerate(order):
@@ -140,7 +150,9 @@
             feat[128 + s * W : 128 + (s + 1) * W, at] = lo
         tail = jnp.concatenate([d * wr, wd[:8] * d[8:], jnp.zeros((8, chunk), F32)], axis=0)
         tail_hi, tail_lo = split(tail)
-        quarter = (lax.shift_right_logical(u, 1) & 3).astype(F32).astype(BF)
+        quarter = jnp.broadcast_to(
+            (lax.shift_right_logical(u, 1) & 3).astype(F32), (32, chunk)
+        ).astype(BF)
         for q in range(4):
             on = quarter == jnp.asarray(q, BF)
             rest_feat[q * 32 : q * 32 + 32, :] = jnp.where(on, tail_hi, zero)
@@ -183,7 +195,7 @@
     lax.fori_loop(0, turns, first_half, 0)
     out_box[:, 4:5] = (rest_acc[:, 0:128] + rest_acc[:, 128:256]).reshape(n, 1, 2, 128)
     fill(0)
-    pl.semaphore_wait(barrier, n - 1 + nt - 1)
+    pl.semaphore_wait(barrier, n - 1 + root_z * ny * (nt - 1))
     send(0)
     lax.fori_loop(0, turns, second_half, 0)
     fill(1)
@@ -244,30 +256,68 @@
     lane_row = lax.broadcasted_iota(jnp.int32, (1, 128), 1)
     plane_msg[...] = jnp.where(lane_row == 0, chi, jnp.where(lane_row == 1, weight_sum, 0.0))
 
-    for m, o in enumerate(order[:-1]):
-        pltpu.make_async_remote_copy(
-            src_ref=plane_msg, dst_ref=plane_in.at[m],
+    def term_copy(d, dy, z):
+        slot = (nt - d) % nt * n + (ny - dy) % ny * nz + (me_z - z + nz) % nz
+        return pltpu.make_async_remote_copy(
+            src_ref=plane_msg, dst_ref=plane_in.at[slot],
             send_sem=plane_send, recv_sem=plane_recv,
-            device_id=peer(o), device_id_type=MESH,
-        ).start()
+            device_id=(ts[d], ys[dy] * nz + z), device_id_type=MESH,
+        )
+
+    ways = sorted(
+        ((d, dy) for d in range(nt) for dy in range(ny)),
+        key=lambda w: -(ring_hops(w[0] // 2, nt // 2) + ring_hops(w[1], ny)),
+    )
+    for d, dy in ways:
+        for z in range(root_z):
+            if (d, dy) != (0, 0):
+                term_copy(d, dy, z).start()
+    for z in range(root_z):
+
+        @pl.when(me_z != z)
+        def _():
+            term_copy(0, 0, z).start()
+
     for k in range(W):
         table[k : k + 1, 0:OWN] = x[k]
     sol_ref[...] = table[...].T[0:OWN, 0:W]
-    pltpu.make_async_copy(plane_in, plane_in, plane_recv).wait()
-    tm_msg[...] = plane_msg[...] + jnp.sum(plane_in[...], axis=0)
-    for d in range(1, nt):
-        pltpu.make_async_remote_copy(
-            src_ref=tm_msg, dst_ref=tm_in.at[d - 1],
+    every = n * nt - 1
+    to_roots = root_z * ny * nt
+
+    def total_copy(i):
+        z = me_z * (root_z + i) + (1 - me_z) * (nz - 1 - i)
+        return pltpu.make_async_remote_copy(
+            src_ref=tm_msg, dst_ref=tm_in,
             send_sem=tm_send, recv_sem=tm_recv,
-            device_id=(ts[d], me_s), device_id_type=MESH,
-        ).start()
+            device_id=(me_t, me_y * nz + z), device_id_type=MESH,
+        )
+
+    def finish(total):
+        misfit_ref[0, 0] = jnp.sum(total[:, 0:1] / total[:, 1:2])
+
+    def drain(count, sem):
+        pltpu.make_async_copy(plane_in.at[0:count], plane_in.at[0:count], sem).wait()
+
+    @pl.when(is_root)
+    def _():
+        drain(every, plane_recv)
+        plane_in[0] = plane_msg[...]
+        total = jnp.sum(plane_in[...], axis=0)
+        tm_msg[...] = total
+        for i in range(served):
+            total_copy(i).start()
+        finish(total)
+        drain(to_roots - 1, plane_send)
+        drain(served, tm_send)
+
+    @pl.when(jnp.logical_not(is_root))
+    def _():
+        pltpu.make_async_copy(tm_in, tm_in, tm_recv).wait()
+        finish(tm_in[...])
+        drain(to_roots, plane_send)
+
     for h in range(2):
         pltpu.make_async_copy(halves[h], halves[h], box_send.at[h]).wait()
-    pltpu.make_async_copy(plane_in, plane_in, plane_send).wait()
-    pltpu.make_async_copy(tm_in, tm_in, tm_recv).wait()
-    total = tm_msg[...] + jnp.sum(tm_in[...], axis=0)
-    misfit_ref[...] = total[:, 0:1] / total[:, 1:2]
-    pltpu.make_async_copy(tm_in, tm_in, tm_send).wait()
 
 
 def solution(mesh):
@@ -279,7 +329,7 @@
 
     def on_device(design, unit_index, residual, weight, obs_count, damping):
         slots = design.shape[1]
-        chunk = min(2048, slots // 2)
+        chunk = min(4096, slots // 2)
         dims = (nt, ny, nz, units, slots, chunk)
         vmem = pl.BlockSpec(memory_space=pltpu.VMEM)
         hbm = pl.BlockSpec(memory_space=pl.ANY)
@@ -288,10 +338,10 @@
             functools.partial(kernel, dims),
             out_shape=(
                 pltpu.VMEM((OWN, W), F32),
-                pltpu.VMEM((1, 1), F32),
+                pltpu.SMEM((1, 1), F32),
             ),
             in_specs=[hbm] * 6,
-            out_specs=(vmem, vmem),
+            out_specs=(vmem, pl.BlockSpec(memory_space=pltpu.SMEM)),
             scratch_shapes=[
                 pltpu.VMEM((W, slots), F32),
                 pltpu.VMEM((1, slots), jnp.int32),
@@ -311,9 +361,9 @@
                 pltpu.VMEM((n, 5, 2, 128), F32),
                 pltpu.VMEM((152, 128), F32),
                 pltpu.VMEM((1, 128), F32),
-                pltpu.VMEM((n - 1, 1, 128), F32),
+                pltpu.VMEM((n * nt, 1, 128), F32),
                 pltpu.VMEM((1, 128), F32),
-                pltpu.VMEM((nt - 1, 1, 128), F32),
+                pltpu.VMEM((1, 128), F32),
                 dma((slots // chunk,)),
                 dma((5,)),
                 dma((2,)),

time: 43.8 us -> 41.3 us (0.943)
  Pallas kernels: 40.6 us -> 38.8 us
  between operations: 2.45 us -> 1.8 us
    pallas_call x1, Pallas kernels: 40.6 us -> 38.8 us  [on_device(): pl.pallas_call(functools.partial(kernel, dims), out_shape=(pltpu.VMEM((OW...]
where the time goes in v3:
time: 41.3 us; the launch traced here: 41.2 us
  Pallas kernels  38.8 us (94%)
  between operations  1.8 us (4%)
  local copies, waits for them, and re-layouts  0.6 us (1%)
    pallas_call x1, Pallas kernels, on_device(): pl.pallas_call(functools.partial(kernel, dims), out_shape=(pltpu.VMEM((OW...  38.8 us

profile of v3, /device:TPU:1, one launch (start us, length us, event | category | flops | bytes accessed | tf_op | source)
XLA Modules:
  0.0 41.2 jit_solution(12758942941595326791)
XLA Ops:
  1.3 38.8 %calibrate.1 = (f32[8,16]{1,0:T(8,128)S(1)}, f32[1,1]{1,0:T(1,128)S(4)}) custom-call(f32[16,16384]{1,0:T(8,128)} %design_hbm.1, s32[1,16384]{1,0:T(1,128)} %bitcast.7, f32[1,16384]{1,0:T(1,128)} %bitcast.8, f32[1,16384]{1,0:T(1,128)} %bitcast.9, s32[1]{0:T(128)S(6)} %copy.12.count_hbm, f32[1,8]{1,0:T(1,128)} %bitcast.10), custom_call_target="tpu_custom_call" | custom-call | tf_op jit(solution)/shard_map/calibrate/pallas_call | solution.py:337
  40.6 0.6 %copy.10 = f32[16,8]{0,1:T(8,128)} copy(f32[16,8]{0,1:T(8,128)S(1)} %bitcast.6) | data formatting | bytes 1024

commit v4 on v3

--- a/solution.py
+++ b/solution.py
@@ -32,6 +32,12 @@
     if s == 8:
         return True, W + i
     return False, (W - s) * W + j
+
+
+def tree_sum(parts):
+    while len(parts) > 1:
+        parts = [sum(parts[i : i + 2][1:], parts[i]) for i in range(0, len(parts), 2)]
+    return parts[0]
 
 
 def kernel(
@@ -148,15 +154,15 @@
             hi, lo = split(wd * turned)
             feat[s * W : (s + 1) * W, at] = hi
             feat[128 + s * W : 128 + (s + 1) * W, at] = lo
-        tail = jnp.concatenate([d * wr, wd[:8] * d[8:], jnp.zeros((8, chunk), F32)], axis=0)
+        tail = jnp.concatenate([d * wr, wd[:8] * d[8:]], axis=0)
         tail_hi, tail_lo = split(tail)
         quarter = jnp.broadcast_to(
-            (lax.shift_right_logical(u, 1) & 3).astype(F32), (32, chunk)
+            (lax.shift_right_logical(u, 1) & 3).astype(F32), (24, chunk)
         ).astype(BF)
         for q in range(4):
             on = quarter == jnp.asarray(q, BF)
-            rest_feat[q * 32 : q * 32 + 32, :] = jnp.where(on, tail_hi, zero)
-            rest_feat[128 + q * 32 : 160 + q * 32, :] = jnp.where(on, tail_lo, zero)
+            rest_feat[q * 24 : q * 24 + 24, :] = jnp.where(on, tail_hi, zero)
+            rest_feat[96 + q * 24 : 120 + q * 24, :] = jnp.where(on, tail_lo, zero)
 
         code = u - 256
         unit_ref[:, at] = code
@@ -164,7 +170,7 @@
             hits(lines[0:half_units, :], code), feat[:, at], dn, preferred_element_type=F32
         )
         rest_code = (lax.shift_right_logical(u, 3) * 2) | (u & 1)
-        rest_acc[...] += lax.dot_general(
+        rest_acc[:, 0:192] += lax.dot_general(
             hits(rest_lines[...], rest_code), rest_feat[...], dn, preferred_element_type=F32
         )
         return carry
@@ -193,7 +199,9 @@
     halves = (in_box.at[0:half_boxes], in_box.at[half_boxes : n - 1])
 
     lax.fori_loop(0, turns, first_half, 0)
-    out_box[:, 4:5] = (rest_acc[:, 0:128] + rest_acc[:, 128:256]).reshape(n, 1, 2, 128)
+    out_box[:, 4:5] = (
+        rest_acc[:, 0:128] + pltpu.roll(rest_acc[...], 160, 1)[:, 0:128]
+    ).reshape(n, 1, 2, 128)
     fill(0)
     pl.semaphore_wait(barrier, n - 1 + root_z * ny * (nt - 1))
     send(0)
@@ -206,9 +214,9 @@
     damping = damping_ref[...]
     own = out_box[n - 1]
     pltpu.make_async_copy(halves[0], halves[0], box_recv.at[0]).wait()
-    own = own + jnp.sum(in_box[0:half_boxes], axis=0)
+    own = tree_sum([own] + [in_box[k] for k in range(half_boxes)])
     pltpu.make_async_copy(halves[1], halves[1], box_recv.at[1]).wait()
-    own = own + jnp.sum(in_box[half_boxes : n - 1], axis=0)
+    own = tree_sum([own] + [in_box[k] for k in range(half_boxes, n - 1)])
     main = own[0:4].reshape(OWN, 128)
     rest = own[4]
     table[0:128, :] = jnp.concatenate([main, jnp.zeros((120, 128), F32)], axis=0).T
@@ -216,7 +224,7 @@
     lane = lax.broadcasted_iota(jnp.int32, (24, 128), 1)
     rest_all = jnp.zeros((24, 128), F32)
     for q in range(4):
-        part = rest_t[q * 32 : q * 32 + 24, :]
+        part = rest_t[q * 24 : q * 24 + 24, :]
         moved = part if q == 0 else pltpu.roll(part, 2 * q, 1)
         rest_all = jnp.where(lane // 2 == q, moved, rest_all)
     table[128:152, :] = rest_all
@@ -259,7 +267,7 @@
     def term_copy(d, dy, z):
         slot = (nt - d) % nt * n + (ny - dy) % ny * nz + (me_z - z + nz) % nz
         return pltpu.make_async_remote_copy(
-            src_ref=plane_msg, dst_ref=plane_in.at[slot],
+            src_ref=plane_msg, dst_ref=plane_in.at[pl.ds(slot, 1)],
             send_sem=plane_send, recv_sem=plane_recv,
             device_id=(ts[d], ys[dy] * nz + z), device_id_type=MESH,
         )
@@ -296,13 +304,14 @@
         misfit_ref[0, 0] = jnp.sum(total[:, 0:1] / total[:, 1:2])
 
     def drain(count, sem):
-        pltpu.make_async_copy(plane_in.at[0:count], plane_in.at[0:count], sem).wait()
+        pltpu.make_async_copy(plane_in.at[pl.ds(0, count)], plane_in.at[pl.ds(0, count)], sem).wait()
 
     @pl.when(is_root)
     def _():
         drain(every, plane_recv)
-        plane_in[0] = plane_msg[...]
-        total = jnp.sum(plane_in[...], axis=0)
+        plane_in[0:1] = plane_msg[...]
+        eights = tree_sum([plane_in[8 * k : 8 * k + 8, :] for k in range(n * nt // 8)])
+        total = jnp.sum(eights, axis=0, keepdims=True)
         tm_msg[...] = total
         for i in range(served):
             total_copy(i).start()
@@ -353,7 +362,7 @@
                 pltpu.VMEM((units, 128), BF),
                 pltpu.VMEM((units // 4, 128), BF),
                 pltpu.VMEM((256, slots), BF),
-                pltpu.VMEM((256, chunk), BF),
+                pltpu.VMEM((192, chunk), BF),
                 pltpu.VMEM((units, 256), F32),
                 pltpu.VMEM((units // 4, 256), F32),
                 pltpu.VMEM((2, chunk), F32),
@@ -361,7 +370,7 @@
                 pltpu.VMEM((n, 5, 2, 128), F32),
                 pltpu.VMEM((152, 128), F32),
                 pltpu.VMEM((1, 128), F32),
-                pltpu.VMEM((n * nt, 1, 128), F32),
+                pltpu.VMEM((n * nt, 128), F32),
                 pltpu.VMEM((1, 128), F32),
                 pltpu.VMEM((1, 128), F32),
                 dma((slots // chunk,)),

time: 41.3 us -> 40.1 us (0.971)
  Pallas kernels: 38.8 us -> 37.6 us
    pallas_call x1, Pallas kernels: 38.8 us -> 37.6 us  [on_device(): pl.pallas_call(functools.partial(kernel, dims), out_shape=(pltpu.VMEM((OW...]
where the time goes in v4:
time: 40.1 us; the launch traced here: 40 us
  Pallas kernels  37.6 us (94%)
  between operations  1.8 us (4%)
  local copies, waits for them, and re-layouts  0.6 us (1%)
    pallas_call x1, Pallas kernels, on_device(): pl.pallas_call(functools.partial(kernel, dims), out_shape=(pltpu.VMEM((OW...  37.6 us

profile of v4, /device:TPU:1, one launch (start us, length us, event | category | flops | bytes accessed | tf_op | source)
XLA Modules:
  0.0 40.0 jit_solution(17799016426735645993)
XLA Ops:
  1.3 37.6 %calibrate.1 = (f32[8,16]{1,0:T(8,128)S(1)}, f32[1,1]{1,0:T(1,128)S(4)}) custom-call(f32[16,16384]{1,0:T(8,128)} %design_hbm.1, s32[1,16384]{1,0:T(1,128)} %bitcast.7, f32[1,16384]{1,0:T(1,128)} %bitcast.8, f32[1,16384]{1,0:T(1,128)} %bitcast.9, s32[1]{0:T(128)S(6)} %copy.12.count_hbm, f32[1,8]{1,0:T(1,128)} %bitcast.10), custom_call_target="tpu_custom_call" | custom-call | tf_op jit(solution)/shard_map/calibrate/pallas_call | solution.py:346
  39.4 0.6 %copy.10 = f32[16,8]{0,1:T(8,128)} copy(f32[16,8]{0,1:T(8,128)S(1)} %bitcast.6) | data formatting | bytes 1024

commit v5 on v4

--- a/solution.py
+++ b/solution.py
@@ -211,6 +211,10 @@
 
     before = jnp.sum(sums_acc[0:1, :], axis=1, keepdims=True)
     weight_sum = jnp.sum(sums_acc[1:2, :], axis=1, keepdims=True)
+    lane_row = lax.broadcasted_iota(jnp.int32, (1, 128), 1)
+    plane_msg[...] = jnp.where(
+        lane_row == OWN, before, jnp.where(lane_row == OWN + 1, weight_sum, 0.0)
+    )
     damping = damping_ref[...]
     own = out_box[n - 1]
     pltpu.make_async_copy(halves[0], halves[0], box_recv.at[0]).wait()
@@ -259,10 +263,7 @@
     for k in range(W):
         gain = gain + x[k] * b0[k]
         square = square + x[k] * x[k]
-    chi = before - jnp.sum(gain + damping * square, axis=1, keepdims=True)
-
-    lane_row = lax.broadcasted_iota(jnp.int32, (1, 128), 1)
-    plane_msg[...] = jnp.where(lane_row == 0, chi, jnp.where(lane_row == 1, weight_sum, 0.0))
+    plane_msg[:, 0:OWN] = -(gain + damping * square)
 
     def term_copy(d, dy, z):
         slot = (nt - d) % nt * n + (ny - dy) % ny * nz + (me_z - z + nz) % nz
@@ -301,7 +302,9 @@
         )
 
     def finish(total):
-        misfit_ref[0, 0] = jnp.sum(total[:, 0:1] / total[:, 1:2])
+        chi = jnp.sum(jnp.where(lane_row <= OWN, total, 0.0), axis=1, keepdims=True)
+        weights = jnp.sum(jnp.where(lane_row == OWN + 1, total, 0.0), axis=1, keepdims=True)
+        misfit_ref[0, 0] = jnp.sum(chi / weights)
 
     def drain(count, sem):
         pltpu.make_async_copy(plane_in.at[pl.ds(0, count)], plane_in.at[pl.ds(0, count)], sem).wait()
@@ -338,7 +341,7 @@
 
     def on_device(design, unit_index, residual, weight, obs_count, damping):
         slots = design.shape[1]
-        chunk = min(4096, slots // 2)
+        chunk = min(8192, slots // 2)
         dims = (nt, ny, nz, units, slots, chunk)
         vmem = pl.BlockSpec(memory_space=pltpu.VMEM)
         hbm = pl.BlockSpec(memory_space=pl.ANY)

time: 40.1 us -> 39.9 us (level)
  no operation moved by 1% of the time
where the time goes in v5:
time: 39.9 us; the launch traced here: 39.8 us
  Pallas kernels  37.4 us (94%)
  between operations  1.8 us (5%)
  local copies, waits for them, and re-layouts  0.6 us (2%)
    pallas_call x1, Pallas kernels, on_device(): pl.pallas_call(functools.partial(kernel, dims), out_shape=(pltpu.VMEM((OW...  37.4 us

profile of v5, /device:TPU:1, one launch (start us, length us, event | category | flops | bytes accessed | tf_op | source)
XLA Modules:
  0.0 39.8 jit_solution(4202403409272099470)
XLA Ops:
  1.3 37.4 %calibrate.1 = (f32[8,16]{1,0:T(8,128)S(1)}, f32[1,1]{1,0:T(1,128)S(4)}) custom-call(f32[16,16384]{1,0:T(8,128)} %design_hbm.1, s32[1,16384]{1,0:T(1,128)} %bitcast.7, f32[1,16384]{1,0:T(1,128)} %bitcast.8, f32[1,16384]{1,0:T(1,128)} %bitcast.9, s32[1]{0:T(128)S(6)} %copy.12.count_hbm, f32[1,8]{1,0:T(1,128)} %bitcast.10), custom_call_target="tpu_custom_call" | custom-call | tf_op jit(solution)/shard_map/calibrate/pallas_call | solution.py:349
  39.2 0.6 %copy.10 = f32[16,8]{0,1:T(8,128)} copy(f32[16,8]{0,1:T(8,128)S(1)} %bitcast.6) | data formatting | bytes 1024

commit v6 on v5

--- a/solution.py
+++ b/solution.py
@@ -73,9 +73,10 @@
             ]
         )
     ]
+    piece(0).start()
     for row in rows:
         row.start()
-    for c in range(turns):
+    for c in range(1, turns):
         piece(c).start()
 
     ys = [(me_y + d) % ny for d in range(ny)]
@@ -294,7 +295,7 @@
     to_roots = root_z * ny * nt
 
     def total_copy(i):
-        z = me_z * (root_z + i) + (1 - me_z) * (nz - 1 - i)
+        z = me_z + 1 + i
         return pltpu.make_async_remote_copy(
             src_ref=tm_msg, dst_ref=tm_in,
             send_sem=tm_send, recv_sem=tm_recv,

time: 39.9 us -> 39.9 us (level)
  no operation moved by 1% of the time
where the time goes in v6:
time: 39.9 us; the launch traced here: 39.8 us
  Pallas kernels  37.4 us (94%)
  between operations  1.8 us (5%)
  local copies, waits for them, and re-layouts  0.6 us (2%)
    pallas_call x1, Pallas kernels, on_device(): pl.pallas_call(functools.partial(kernel, dims), out_shape=(pltpu.VMEM((OW...  37.4 us

profile of v6, /device:TPU:1, one launch (start us, length us, event | category | flops | bytes accessed | tf_op | source)
XLA Modules:
  0.0 39.8 jit_solution(16030360031875888645)
XLA Ops:
  1.3 37.4 %calibrate.1 = (f32[8,16]{1,0:T(8,128)S(1)}, f32[1,1]{1,0:T(1,128)S(4)}) custom-call(f32[16,16384]{1,0:T(8,128)} %design_hbm.1, s32[1,16384]{1,0:T(1,128)} %bitcast.7, f32[1,16384]{1,0:T(1,128)} %bitcast.8, f32[1,16384]{1,0:T(1,128)} %bitcast.9, s32[1]{0:T(128)S(6)} %copy.12.count_hbm, f32[1,8]{1,0:T(1,128)} %bitcast.10), custom_call_target="tpu_custom_call" | custom-call | tf_op jit(solution)/shard_map/calibrate/pallas_call | solution.py:350
  39.2 0.6 %copy.10 = f32[16,8]{0,1:T(8,128)} copy(f32[16,8]{0,1:T(8,128)S(1)} %bitcast.6) | data formatting | bytes 1024
